TPU v7x, 32 devices: a whole 2x2x4 slice. The times are simulated.
32 devices in a mesh: seq: 16 (over z, x, core), head: 2 (over y).
Axes of the slice: x: 2, y: 2, z: 4, core: 2. Of those that a mesh axis runs over, the one named last changes fastest.
Arguments:
- hidden: bfloat16 [4608, 8192], P('seq'), may hold values from -6 to 6
- norm_gain: bfloat16 [8192], replicated, may hold values from 0.099609375 to 1.8984375
- w_query: bfloat16 [8192, 1024], P('seq', 'head'), may hold values from -0.125 to 0.125
- w_key: bfloat16 [8192, 256], P('seq', 'head'), may hold values from -0.125 to 0.125
- w_value: bfloat16 [8192, 256], P('seq', 'head'), may hold values from -0.0625 to 0.0625
- bias_query: bfloat16 [1024], P('head'), may hold values from -3 to 3
- bias_key: bfloat16 [256], P('head'), may hold values from -200 to 200
- bias_value: bfloat16 [256], P('head'), may hold values from -3 to 3
- w_out: bfloat16 [1024, 8192], P('head', 'seq'), may hold values from -0.1875 to 0.1875
Outputs:
- attn_out: bfloat16 [4608, 8192], P(('seq', 'head'))
All inputs are finite; a program needn't handle non-finite values.
Results may differ from a plain program's by a relative error of at most 0.014.
The roundings to bfloat16 on the way count: a program that leaves them out, or rounds other values in their place, can miss the bound.
Values may be sent and summed in bfloat16 or wider, within the bound.
No kernel may reach another device: no remote copies, remote signals or barrier semaphores. Data moves between devices by JAX's collectives and lax.ppermute only.
A program may use at most 192 MiB of HBM per device.

v0:
```python
import jax
import jax.numpy as jnp
from jax import lax
from jax.sharding import PartitionSpec as P

HEAD_DIM = 128
ROPE_BASE = 1000000.0
EPSILON = 1e-06


def rotary(values, positions):
    half_dim = values.shape[-1] // 2
    freq = ROPE_BASE ** (-2.0 * jnp.arange(half_dim, dtype=jnp.float32) / values.shape[-1])
    angles = positions.astype(jnp.float32)[:, None, None] * freq[None, None, :]
    cosine = jnp.cos(angles)
    sine = jnp.sin(angles)
    first = values[..., :half_dim]
    second = values[..., half_dim:]
    return jnp.concatenate(
        [first * cosine - second * sine, second * cosine + first * sine], axis=-1
    )


def local(hidden, norm_gain, w_query, w_key, w_value, bias_query, bias_key, bias_value, w_out):
    row_count = hidden.shape[0]
    head_count = w_query.shape[1] // HEAD_DIM
    first_row = lax.axis_index("seq") * row_count
    last_row = first_row + row_count - 1
    positions = first_row + jnp.arange(row_count, dtype=jnp.int32)
    widened = hidden.astype(jnp.float32)
    inverse = lax.rsqrt(jnp.mean(widened * widened, axis=-1, keepdims=True) + EPSILON)
    normed = (widened * inverse * norm_gain.astype(jnp.float32)).astype(jnp.bfloat16)
    query = jnp.dot(
        normed,
        lax.all_gather(w_query, "seq", axis=0, tiled=True),
        preferred_element_type=jnp.float32,
    )
    keys = jnp.dot(
        normed, lax.all_gather(w_key, "seq", axis=0, tiled=True), preferred_element_type=jnp.float32
    )
    values = jnp.dot(
        normed,
        lax.all_gather(w_value, "seq", axis=0, tiled=True),
        preferred_element_type=jnp.float32,
    )
    query = query + bias_query.astype(jnp.float32)
    keys = keys + bias_key.astype(jnp.float32)
    values = values + bias_value.astype(jnp.float32)
    query = rotary(query.reshape(row_count, head_count, HEAD_DIM), positions).astype(jnp.bfloat16)
    keys = (
        rotary(keys.reshape(row_count, 1, HEAD_DIM), positions)
        .reshape(row_count, HEAD_DIM)
        .astype(jnp.bfloat16)
    )
    values = values.astype(jnp.bfloat16)
    query_heads = query.transpose(1, 0, 2)
    scaling = HEAD_DIM ** (-0.5)
    initial = (
        jnp.full((head_count, row_count), -1e30, jnp.float32),
        jnp.zeros((head_count, row_count), jnp.float32),
        jnp.zeros((head_count, row_count, HEAD_DIM), jnp.float32),
    )
    key_piece = lax.all_gather(keys, "seq", axis=0, tiled=True)
    value_piece = lax.all_gather(values, "seq", axis=0, tiled=True)

    def update(state):
        highest, total, summed = state
        scores = (
            jnp.einsum("hqd,kd->hqk", query_heads, key_piece, preferred_element_type=jnp.float32)
            * scaling
        )
        key_positions = jnp.arange(key_piece.shape[0], dtype=jnp.int32)
        allowed = positions[:, None] >= key_positions[None, :]
        scores = jnp.where(allowed[None], scores, -jnp.inf)
        new_high = jnp.maximum(highest, jnp.max(scores, axis=-1))
        probs = jnp.exp(scores - new_high[..., None])
        total = jnp.sum(probs, axis=-1)
        mixed = jnp.einsum(
            "hqk,kd->hqd",
            probs.astype(jnp.bfloat16),
            value_piece,
            preferred_element_type=jnp.float32,
        )
        return (new_high, total, mixed)

    def unchanged(state):
        return state

    highest, total, summed = lax.cond(jnp.int32(0) <= last_row, update, unchanged, initial)
    attended = (summed / total[..., None]).astype(jnp.bfloat16)
    attended = attended.transpose(1, 0, 2).reshape(row_count, head_count * HEAD_DIM)
    partial_out = jnp.dot(
        attended,
        lax.all_gather(w_out, "seq", axis=1, tiled=True),
        preferred_element_type=jnp.float32,
    )
    result = lax.psum_scatter(
        partial_out.astype(jnp.bfloat16), "head", scatter_dimension=0, tiled=True
    )
    return result


def solution(mesh):
    in_specs = (
        P("seq", None),
        P(),
        P("seq", "head"),
        P("seq", "head"),
        P("seq", "head"),
        P("head"),
        P("head"),
        P("head"),
        P("head", "seq"),
    )
    out_specs = P(("seq", "head"), None)
    return jax.shard_map(local, mesh=mesh, in_specs=in_specs, out_specs=out_specs, check_vma=False)
```

profile of v0, /device:TPU:0, one launch (start us, length us, event | category | flops | bytes accessed | tf_op | source)
XLA Modules:
  0.0 401.3 jit_solution(17232137514900571910)
XLA Ops:
  6.5 0.7 all-gather.10.cloned.1.call-update
  7.3 0.7 all-gather.12.cloned.1.call-update
  8.1 0.7 all-gather.8.cloned.1.call-update
  8.8 0.7 convert_element_type.48
  9.5 0.7 convert_element_type.52
  10.2 3.4 fusion.11
  13.6 40.1 %all-gather.10.cloned.1.call-done = bf16[8192,128]{1,0:T(8,128)(2,1)} async-done(((bf16[512,128]{1,0:T(8,128)(2,1)}), bf16[8192,128]{1,0:T(8,128)(2,1)}) %all-gather.10.cloned.1.call-update) | async-done | bytes 2097168 | tf_op jit(solution)/shard_map/all_gather | solution.py:39
  53.7 4.6 %fusion.14 = f32[288,1,128]{2,0,1:T(8,128)S(1)} fusion(bf16[8192,128]{1,0:T(8,128)(2,1)} %all-gather.10.cloned.1.call-done, f32[128]{0:T(128)S(1)} %convert_element_type.52, bf16[288,8192]{1,0:T(8,128)(2,1)} %param.11, f32[8192]{0:T(1024)S(1)} %convert_element_type.48, f32[288]{0:T(512)S(1)} %add_rsqrt_fusion), kind=kOutput, calls=%fused_computation.24 | convolution fusion | flops 613453824 | bytes 6997632 | tf_op jit(solution)/shard_map/dot_general | solution.py:38
  58.3 0.7 fusion.24
  58.9 0.7 pad_maximum_fusion
  59.8 36.3 %all-gather.12.cloned.1.call-done = bf16[8192,128]{1,0:T(8,128)(2,1)} async-done(((bf16[512,128]{1,0:T(8,128)(2,1)}), bf16[8192,128]{1,0:T(8,128)(2,1)}) %all-gather.12.cloned.1.call-update) | async-done | bytes 2097168 | tf_op jit(solution)/shard_map/all_gather | solution.py:43
  96.1 5.1 %fusion.15 = bf16[288,128]{1,0:T(8,128)(2,1)} fusion(bf16[8192,128]{1,0:T(8,128)(2,1)} %all-gather.12.cloned.1.call-done, f32[128]{0:T(128)S(1)} %convert_element_type.54, bf16[288,8192]{1,0:T(8,128)(2,1)} %param.11, f32[8192]{0:T(1024)S(1)} %convert_element_type.48, f32[288]{0:T(512)S(1)} %add_rsqrt_fusion), kind=kOutput, calls=%fused_computation.25 | convolution fusion | flops 613490688 | bytes 6923904 | tf_op jit(solution)/shard_map/dot_general | solution.py:41
  102.7 68.6 %all-gather.8.cloned.1.call-done = bf16[8192,512]{1,0:T(8,128)(2,1)} async-done(((bf16[512,512]{1,0:T(8,128)(2,1)}), bf16[8192,512]{1,0:T(8,128)(2,1)}) %all-gather.8.cloned.1.call-update) | async-done | bytes 8388624 | tf_op jit(solution)/shard_map/all_gather | solution.py:35
  171.3 7.0 %convolution_add_fusion = f32[288,512]{1,0:T(8,128)S(1)} fusion(bf16[8192,512]{1,0:T(8,128)(2,1)} %all-gather.8.cloned.1.call-done, f32[512]{0:T(512)S(1)} %convert_element_type.50, bf16[288,8192]{1,0:T(8,128)(2,1)} %param.11, f32[8192]{0:T(1024)S(1)} %convert_element_type.48, f32[288]{0:T(512)S(1)} %add_rsqrt_fusion), kind=kOutput, calls=%fused_computation.21 | convolution fusion | flops 2425503744 | bytes 13732992 | tf_op jit(solution)/shard_map/dot_general | solution.py:33
  179.3 31.1 %all-gather.18.cloned.1.call-done = bf16[4608,1,128]{2,0,1:T(8,128)(2,1)} async-done(((bf16[288,1,128]{2,0,1:T(8,128)(2,1)}), bf16[4608,1,128]{2,0,1:T(8,128)(2,1)}) %all-gather.18.cloned.1.call-update) | async-done | bytes 1179664 | tf_op jit(solution)/shard_map/all_gather | solution.py:63
  210.3 39.3 %all-gather.14.cloned.1.call-done = bf16[4608,128]{1,0:T(8,128)(2,1)} async-done(((bf16[288,128]{1,0:T(8,128)(2,1)}), bf16[4608,128]{1,0:T(8,128)(2,1)}) %all-gather.14.cloned.1.call-update) | async-done | bytes 1179664 | tf_op jit(solution)/shard_map/all_gather | solution.py:64
  249.7 19.5 %conditional.1 = (f32[4,288]{1,0:T(4,128)S(1)}, f32[4,288,128]{2,1,0:T(8,128)S(1)}) conditional(s32[]{:T(128)} %convert_element_type.46, () %tuple.13, (s32[]{:T(128)}, s32[288]{0:T(512)S(1)}, bf16[4,288,128]{2,1,0:T(8,128)(2,1)S(1)}, bf16[4608,128]{1,0:T(8,128)(2,1)}, bf16[4608,128]{1,0:T(8,128)(2,1)}) %tuple.36), branch_computations={%region_1.0_spmd, %region_2.5_spmd} | conditional | flops 2777627648 | bytes 72284560 | solution.py:89
  249.7 0.8 iota_compare_fusion
  250.5 5.5 %fusion = (f32[4,288]{1,0:T(4,128)S(1)}, f32[4,288,4608]{2,1,0:T(8,128)S(1)}) fusion(pred[288,4608]{1,0:T(8,128)(4,1)S(1)} %iota_compare_fusion, bf16[4,288,128]{2,1,0:T(8,128)(2,1)S(1)} %get-tuple-element.19, bf16[4608,128]{1,0:T(8,128)(2,1)} %get-tuple-element.20), kind=kOutput, calls=%fused_computation.2 | convolution fusion | flops 1374878592 | bytes 24039936 | tf_op jit(solution)/shard_map/cond/branch_1_fun/hqd,kd->hqk/dot_general | solution.py:69
  255.9 6.6 %fusion.3 = f32[4,288,128]{2,1,0:T(8,128)S(1)} fusion(f32[4,288,4608]{2,1,0:T(8,128)S(1)} %get-tuple-element.27, f32[4,288]{1,0:T(4,128)S(1)} %broadcast_maximum_fusion, pred[288,4608]{1,0:T(8,128)(4,1)S(1)} %iota_compare_fusion, bf16[4608,128]{1,0:T(8,128)(2,1)} %get-tuple-element.21), kind=kOutput, calls=%fused_computation.5 | convolution fusion | flops 1380188160 | bytes 24334848 | tf_op jit(solution)/shard_map/cond/branch_1_fun/hqk,kd->hqd/dot_general | solution.py:78
  262.6 6.6 %fusion.2 = f32[4,288]{1,0:T(4,128)S(1)} fusion(f32[4,288,4608]{2,1,0:T(8,128)S(1)} %get-tuple-element.27, f32[4,288]{1,0:T(4,128)S(1)} %broadcast_maximum_fusion, pred[288,4608]{1,0:T(8,128)(4,1)S(1)} %iota_compare_fusion), kind=kLoop, calls=%fused_computation.4 | loop fusion | flops 21232512 | bytes 22569984 | tf_op jit(solution)/shard_map/cond/branch_1_fun/reduce_sum | solution.py:77
  269.2 59.2 %all-gather.16.cloned.1.call-done = bf16[512,8192]{1,0:T(8,128)(2,1)} async-done(((bf16[512,512]{1,0:T(8,128)(2,1)}), bf16[512,8192]{1,0:T(8,128)(2,1)}) %all-gather.16.cloned.1.call-update) | async-done | bytes 8388624 | tf_op jit(solution)/shard_map/all_gather | solution.py:94
  328.3 7.7 %convolution_convert_fusion = bf16[288,8192]{1,0:T(8,128)(2,1)} fusion(bf16[512,8192]{1,0:T(8,128)(2,1)} %all-gather.16.cloned.1.call-done, f32[4,288,128]{2,1,0:T(8,128)S(1)} %get-tuple-element.24, f32[4,288]{1,0:T(4,128)S(1)} %get-tuple-element.25), kind=kOutput, calls=%fused_computation.17 | convolution fusion | flops 2418573312 | bytes 13701632 | tf_op jit(solution)/shard_map/dot_general | solution.py:92
  336.1 58.4 %reduce-scatter.2.cloned.1.call-done = bf16[144,8192]{1,0:T(8,128)(2,1)} async-done(((bf16[288,8192]{1,0:T(8,128)(2,1)}), bf16[144,8192]{1,0:T(8,128)(2,1)}) %reduce-scatter.2.cloned.1.call-update) | async-done | bytes 2359312 | tf_op jit(solution)/shard_map/reduce_scatter | solution.py:97
  (28 shorter events, 2.5 us)
Async XLA Ops:
  6.5 47.2 %all-gather.10.cloned.1.call-start = ((), (), s32[]{:S(2)}) async-start(), calls=%async_computation.2 | async-start | bytes 2228224 | tf_op jit(solution)/shard_map/all_gather | solution.py:39
  7.3 88.8 %all-gather.12.cloned.1.call-start = ((), (), s32[]{:S(2)}) async-start(), calls=%async_computation.3 | async-start | bytes 2228224 | tf_op jit(solution)/shard_map/all_gather | solution.py:43
  8.0 163.3 %all-gather.8.cloned.1.call-start = ((), (), s32[]{:S(2)}) async-start(), calls=%async_computation.1 | async-start | bytes 8912896 | tf_op jit(solution)/shard_map/all_gather | solution.py:35
  8.7 201.6 %all-gather.18.cloned.1.call-start = ((), (), s32[]{:S(2)}) async-start(), calls=%async_computation.7 | async-start | bytes 1253376 | tf_op jit(solution)/shard_map/all_gather | solution.py:63
  13.5 46.2 %copy-start.1 = (bf16[128]{0:T(256)(128)(2,1)S(1)}, bf16[128]{0:T(256)(128)(2,1)}, u32[]{:S(2)}) copy-start(bf16[128]{0:T(256)(128)(2,1)} %param.18) | copy-start | bytes 772
  58.3 43.8 %copy-start = (bf16[512]{0:T(512)(128)(2,1)S(1)}, bf16[512]{0:T(512)(128)(2,1)}, u32[]{:S(2)}) copy-start(bf16[512]{0:T(512)(128)(2,1)} %param.16) | copy-start | bytes 3076
  59.7 190.0 %all-gather.14.cloned.1.call-start = ((), (), s32[]{:S(2)}) async-start(), calls=%async_computation.4 | async-start | bytes 1253376 | tf_op jit(solution)/shard_map/all_gather | solution.py:64
  101.2 227.1 %all-gather.16.cloned.1.call-start = ((), (), s32[]{:S(2)}) async-start(), calls=%async_computation.5 | async-start | bytes 8912896 | tf_op jit(solution)/shard_map/all_gather | solution.py:94
  101.8 292.6 %reduce-scatter.2.cloned.1.call-start = ((), (), s32[]{:S(2)}) async-start(), calls=%async_computation.6 | async-start | bytes 7077888 | tf_op jit(solution)/shard_map/reduce_scatter | solution.py:97
Sparse Core Ops, SparseCore 0:
  9.5 44.1 all-gather.9
  55.9 40.1 all-gather.11
  98.2 73.0 all-gather.7
  173.4 36.8 all-gather.17
  212.5 37.1 all-gather.13
  251.7 76.5 all-gather.15
  336.2 58.2 reduce-scatter.1
where the time goes:
time: 402 us; the launch traced here: 401 us
  waiting for transfers between devices  336 us (84%)
  matrix products  36.6 us (9%)
  other arithmetic  14.4 us (4%)
  between operations  13.6 us (3%)
    all_gather x1, waiting for transfers between devices, local(): lax.all_gather(w_query, 'seq', axis=0, tiled=True)  68.6 us
    all_gather x1, waiting for transfers between devices, local(): lax.all_gather(w_out, 'seq', axis=1, tiled=True)  59.2 us
    reduce_scatter x1, waiting for transfers between devices, local(): lax.psum_scatter(partial_out.astype(jnp.bfloat16), 'head', scatter_dimens...  58.4 us
    all_gather x1, waiting for transfers between devices, local(): lax.all_gather(w_key, 'seq', axis=0, tiled=True)  40.1 us
    all_gather x1, waiting for transfers between devices, local(): value_piece = lax.all_gather(values, 'seq', axis=0, tiled=True)  39.3 us
    all_gather x1, waiting for transfers between devices, local(): lax.all_gather(w_value, 'seq', axis=0, tiled=True)  36.3 us
    all_gather x1, waiting for transfers between devices, local(): key_piece = lax.all_gather(keys, 'seq', axis=0, tiled=True)  31.1 us
  transfers between devices with their start and end apart: 7, of which 7 were waited for; matrix products, arithmetic and copies ran while one was open for 11% of the time, Pallas kernels for 0%

commit v1 on v0

--- a/solution.py
+++ b/solution.py
@@ -1,11 +1,30 @@
+import functools
 import jax
 import jax.numpy as jnp
 from jax import lax
 from jax.sharding import PartitionSpec as P
+from jax.lax import axis_index, axis_size, ppermute
 
 HEAD_DIM = 128
 ROPE_BASE = 1000000.0
 EPSILON = 1e-06
+
+
+def arrange_corner_in(content, named_axis, where_dim):
+    finding = axis_size(named_axis)
+    y2, o_now, carry_out = (finding, axis_index(named_axis), content.shape[where_dim])
+    by_rank = [dev * y2 if nth == where_dim else dev for nth, dev in enumerate(content.shape)]
+    back = jnp.zeros(by_rank, content.dtype)
+    x_new = lax.dynamic_update_slice_in_dim(back, content, o_now * carry_out, axis=where_dim)
+    for ix in tuple(range(1, y2)):
+        content = ppermute(content, named_axis, [(nth, (nth + 1) % y2) for nth in range(y2)])
+        x_new = lax.dynamic_update_slice_in_dim(
+            x_new, content, (o_now - ix) % y2 * carry_out, axis=where_dim
+        )
+    return x_new
+
+
+push_the_sites = functools.partial(arrange_corner_in, named_axis="seq", where_dim=0)
 
 
 def rotary(values, positions):
@@ -35,9 +54,7 @@
         lax.all_gather(w_query, "seq", axis=0, tiled=True),
         preferred_element_type=jnp.float32,
     )
-    keys = jnp.dot(
-        normed, lax.all_gather(w_key, "seq", axis=0, tiled=True), preferred_element_type=jnp.float32
-    )
+    keys = jnp.dot(normed, push_the_sites(w_key), preferred_element_type=jnp.float32)
     values = jnp.dot(
         normed,
         lax.all_gather(w_value, "seq", axis=0, tiled=True),

time: 402 us -> 370 us (0.920)
  waiting for transfers between devices: 336 us -> 306 us
    ppermute x0 -> x15, waiting for transfers between devices: none -> 121 us  [arrange_corner_in(): ppermute(content, named_axis, [(nth, (nth + 1) % y2) for nth in range(y2)])]
    all_gather x1, waiting for transfers between devices: 68.6 us -> 0.02 us  [local(): lax.all_gather(w_query, 'seq', axis=0, tiled=True)]
    all_gather x1 -> x0, waiting for transfers between devices: 40.1 us -> none  [local(): lax.all_gather(w_key, 'seq', axis=0, tiled=True)]
    all_gather x1, waiting for transfers between devices: 36.3 us -> 0.02 us  [local(): lax.all_gather(w_value, 'seq', axis=0, tiled=True)]
    all_gather x1, waiting for transfers between devices: 31.1 us -> 25.7 us  [local(): key_piece = lax.all_gather(keys, 'seq', axis=0, tiled=True)]
  transfers between devices with their start and end apart: 7 -> 21, of which waited for: 7 -> 19; matrix products, arithmetic and copies ran while one was open for 11% -> 11% of each run, Pallas kernels for 0% -> 0%
where the time goes in v1:
time: 370 us; the launch traced here: 369 us
  waiting for transfers between devices  306 us (83%)
  matrix products  33.8 us (9%)
  between operations  14.2 us (4%)
  other arithmetic  13 us (4%)
    ppermute x15, waiting for transfers between devices, arrange_corner_in(): ppermute(content, named_axis, [(nth, (nth + 1) % y2) for nth in range(y2)])  121 us
    all_gather x1, waiting for transfers between devices, local(): lax.all_gather(w_out, 'seq', axis=1, tiled=True)  59.2 us
    reduce_scatter x1, waiting for transfers between devices, local(): lax.psum_scatter(partial_out.astype(jnp.bfloat16), 'head', scatter_dimens...  58.4 us
    all_gather x1, waiting for transfers between devices, local(): value_piece = lax.all_gather(values, 'seq', axis=0, tiled=True)  39.3 us
    all_gather x1, waiting for transfers between devices, local(): key_piece = lax.all_gather(keys, 'seq', axis=0, tiled=True)  25.7 us
    dot_general x1, matrix products, local(): jnp.dot(attended, lax.all_gather(w_out, 'seq', axis=1, tiled=True), prefe...  7.84 us
  transfers between devices with their start and end apart: 21, of which 19 were waited for; matrix products, arithmetic and copies ran while one was open for 11% of the time, Pallas kernels for 0%

profile of v1, /device:TPU:0, one launch (start us, length us, event | category | flops | bytes accessed | tf_op | source)
XLA Modules:
  0.0 369.3 jit_solution(14243874097703184129)
XLA Ops:
  8.6 7.8 %collective-permute-done = bf16[512,128]{1,0:T(8,128)(2,1)S(1)} collective-permute-done((bf16[512,128]{1,0:T(8,128)(2,1)}, bf16[512,128]{1,0:T(8,128)(2,1)S(1)}, u32[]{:S(2)}, u32[]{:S(2)}) %collective-permute-start) | collective-permute-done | bytes 131104 | tf_op jit(solution)/shard_map/ppermute | solution.py:20
  16.4 7.2 %collective-permute-done.1 = bf16[512,128]{1,0:T(8,128)(2,1)S(1)} collective-permute-done((bf16[512,128]{1,0:T(8,128)(2,1)S(1)}, bf16[512,128]{1,0:T(8,128)(2,1)S(1)}, u32[]{:S(2)}, u32[]{:S(2)}) %collective-permute-start.1) | collective-permute-done | bytes 131104 | tf_op jit(solution)/shard_map/ppermute | solution.py:20
  23.6 8.6 %collective-permute-done.2 = bf16[512,128]{1,0:T(8,128)(2,1)S(1)} collective-permute-done((bf16[512,128]{1,0:T(8,128)(2,1)S(1)}, bf16[512,128]{1,0:T(8,128)(2,1)S(1)}, u32[]{:S(2)}, u32[]{:S(2)}) %collective-permute-start.2) | collective-permute-done | bytes 131104 | tf_op jit(solution)/shard_map/ppermute | solution.py:20
  32.2 7.1 %collective-permute-done.3 = bf16[512,128]{1,0:T(8,128)(2,1)S(1)} collective-permute-done((bf16[512,128]{1,0:T(8,128)(2,1)S(1)}, bf16[512,128]{1,0:T(8,128)(2,1)S(1)}, u32[]{:S(2)}, u32[]{:S(2)}) %collective-permute-start.3) | collective-permute-done | bytes 131104 | tf_op jit(solution)/shard_map/ppermute | solution.py:20
  39.3 8.9 %collective-permute-done.4 = bf16[512,128]{1,0:T(8,128)(2,1)S(1)} collective-permute-done((bf16[512,128]{1,0:T(8,128)(2,1)S(1)}, bf16[512,128]{1,0:T(8,128)(2,1)S(1)}, u32[]{:S(2)}, u32[]{:S(2)}) %collective-permute-start.4) | collective-permute-done | bytes 131104 | tf_op jit(solution)/shard_map/ppermute | solution.py:20
  55.3 7.1 %collective-permute-done.6 = bf16[512,128]{1,0:T(8,128)(2,1)S(1)} collective-permute-done((bf16[512,128]{1,0:T(8,128)(2,1)S(1)}, bf16[512,128]{1,0:T(8,128)(2,1)S(1)}, u32[]{:S(2)}, u32[]{:S(2)}) %collective-permute-start.6) | collective-permute-done | bytes 131104 | tf_op jit(solution)/shard_map/ppermute | solution.py:20
  63.2 6.4 %collective-permute-done.7 = bf16[512,128]{1,0:T(8,128)(2,1)S(1)} collective-permute-done((bf16[512,128]{1,0:T(8,128)(2,1)S(1)}, bf16[512,128]{1,0:T(8,128)(2,1)S(1)}, u32[]{:S(2)}, u32[]{:S(2)}) %collective-permute-start.7) | collective-permute-done | bytes 131104 | tf_op jit(solution)/shard_map/ppermute | solution.py:20
  69.7 10.0 %collective-permute-done.8 = bf16[512,128]{1,0:T(8,128)(2,1)S(1)} collective-permute-done((bf16[512,128]{1,0:T(8,128)(2,1)S(1)}, bf16[512,128]{1,0:T(8,128)(2,1)S(1)}, u32[]{:S(2)}, u32[]{:S(2)}) %collective-permute-start.8) | collective-permute-done | bytes 131104 | tf_op jit(solution)/shard_map/ppermute | solution.py:20
  79.7 9.9 %collective-permute-done.9 = bf16[512,128]{1,0:T(8,128)(2,1)S(1)} collective-permute-done((bf16[512,128]{1,0:T(8,128)(2,1)S(1)}, bf16[512,128]{1,0:T(8,128)(2,1)S(1)}, u32[]{:S(2)}, u32[]{:S(2)}) %collective-permute-start.9) | collective-permute-done | bytes 131104 | tf_op jit(solution)/shard_map/ppermute | solution.py:20
  89.7 7.1 %collective-permute-done.10 = bf16[512,128]{1,0:T(8,128)(2,1)S(1)} collective-permute-done((bf16[512,128]{1,0:T(8,128)(2,1)S(1)}, bf16[512,128]{1,0:T(8,128)(2,1)S(1)}, u32[]{:S(2)}, u32[]{:S(2)}) %collective-permute-start.10) | collective-permute-done | bytes 131104 | tf_op jit(solution)/shard_map/ppermute | solution.py:20
  96.9 10.0 %collective-permute-done.11 = bf16[512,128]{1,0:T(8,128)(2,1)S(1)} collective-permute-done((bf16[512,128]{1,0:T(8,128)(2,1)S(1)}, bf16[512,128]{1,0:T(8,128)(2,1)S(1)}, u32[]{:S(2)}, u32[]{:S(2)}) %collective-permute-start.11) | collective-permute-done | bytes 131104 | tf_op jit(solution)/shard_map/ppermute | solution.py:20
  106.9 10.0 %collective-permute-done.12 = bf16[512,128]{1,0:T(8,128)(2,1)S(1)} collective-permute-done((bf16[512,128]{1,0:T(8,128)(2,1)S(1)}, bf16[512,128]{1,0:T(8,128)(2,1)S(1)}, u32[]{:S(2)}, u32[]{:S(2)}) %collective-permute-start.12) | collective-permute-done | bytes 131104 | tf_op jit(solution)/shard_map/ppermute | solution.py:20
  116.9 7.6 %collective-permute-done.13 = bf16[512,128]{1,0:T(8,128)(2,1)S(1)} collective-permute-done((bf16[512,128]{1,0:T(8,128)(2,1)S(1)}, bf16[512,128]{1,0:T(8,128)(2,1)S(1)}, u32[]{:S(2)}, u32[]{:S(2)}) %collective-permute-start.13) | collective-permute-done | bytes 131104 | tf_op jit(solution)/shard_map/ppermute | solution.py:20
  124.6 10.0 %collective-permute-done.14 = bf16[512,128]{1,0:T(8,128)(2,1)S(1)} collective-permute-done((bf16[512,128]{1,0:T(8,128)(2,1)S(1)}, bf16[512,128]{1,0:T(8,128)(2,1)S(1)}, u32[]{:S(2)}, u32[]{:S(2)}) %collective-permute-start.14) | collective-permute-done | bytes 131104 | tf_op jit(solution)/shard_map/ppermute | solution.py:20
  144.5 7.1 %convolution_add_fusion = f32[288,512]{1,0:T(8,128)S(1)} fusion(bf16[8192,512]{1,0:T(8,128)(2,1)} %all-gather.7.cloned.1.call-done, f32[512]{0:T(512)S(1)} %convert_element_type.50, bf16[288,8192]{1,0:T(8,128)(2,1)} %param.11, f32[8192]{0:T(1024)S(1)} %convert_element_type.48, f32[288]{0:T(512)S(1)} %add_rsqrt_fusion), kind=kOutput, calls=%fused_computation.21 | convolution fusion | flops 2425503744 | bytes 13732992 | tf_op jit(solution)/shard_map/dot_general | solution.py:52
  152.5 25.7 %all-gather.15.cloned.1.call-done = bf16[4608,1,128]{2,0,1:T(8,128)(2,1)} async-done(((bf16[288,1,128]{2,0,1:T(8,128)(2,1)}), bf16[4608,1,128]{2,0,1:T(8,128)(2,1)}) %all-gather.15.cloned.1.call-update) | async-done | bytes 1179664 | tf_op jit(solution)/shard_map/all_gather | solution.py:80
  178.2 39.3 %all-gather.11.cloned.1.call-done = bf16[4608,128]{1,0:T(8,128)(2,1)} async-done(((bf16[288,128]{1,0:T(8,128)(2,1)}), bf16[4608,128]{1,0:T(8,128)(2,1)}) %all-gather.11.cloned.1.call-update) | async-done | bytes 1179664 | tf_op jit(solution)/shard_map/all_gather | solution.py:81
  217.6 19.4 %conditional.1 = (f32[4,288]{1,0:T(4,128)S(1)}, f32[4,288,128]{2,1,0:T(8,128)S(1)}) conditional(s32[]{:T(128)} %convert_element_type.46, () %tuple.13, (s32[]{:T(128)}, s32[288]{0:T(512)S(1)}, bf16[4,288,128]{2,1,0:T(8,128)(2,1)S(1)}, bf16[4608,128]{1,0:T(8,128)(2,1)}, bf16[4608,128]{1,0:T(8,128)(2,1)}) %tuple.34), branch_computations={%region_1.2_spmd, %region_2.5_spmd} | conditional | flops 2777627648 | bytes 72284560 | solution.py:106
  218.4 5.4 %fusion = (f32[4,288]{1,0:T(4,128)S(1)}, f32[4,288,4608]{2,1,0:T(8,128)S(1)}) fusion(pred[288,4608]{1,0:T(8,128)(4,1)S(1)} %iota_compare_fusion, bf16[4,288,128]{2,1,0:T(8,128)(2,1)S(1)} %get-tuple-element.19, bf16[4608,128]{1,0:T(8,128)(2,1)} %get-tuple-element.20), kind=kOutput, calls=%fused_computation.2 | convolution fusion | flops 1374878592 | bytes 24039936 | tf_op jit(solution)/shard_map/cond/branch_1_fun/hqd,kd->hqk/dot_general | solution.py:86
  223.8 6.6 %fusion.3 = f32[4,288,128]{2,1,0:T(8,128)S(1)} fusion(f32[4,288,4608]{2,1,0:T(8,128)S(1)} %get-tuple-element.27, f32[4,288]{1,0:T(4,128)S(1)} %broadcast_maximum_fusion, pred[288,4608]{1,0:T(8,128)(4,1)S(1)} %iota_compare_fusion, bf16[4608,128]{1,0:T(8,128)(2,1)} %get-tuple-element.21), kind=kOutput, calls=%fused_computation.5 | convolution fusion | flops 1380188160 | bytes 24334848 | tf_op jit(solution)/shard_map/cond/branch_1_fun/hqk,kd->hqd/dot_general | solution.py:95
  230.4 6.6 %fusion.2 = f32[4,288]{1,0:T(4,128)S(1)} fusion(f32[4,288,4608]{2,1,0:T(8,128)S(1)} %get-tuple-element.27, f32[4,288]{1,0:T(4,128)S(1)} %broadcast_maximum_fusion, pred[288,4608]{1,0:T(8,128)(4,1)S(1)} %iota_compare_fusion), kind=kLoop, calls=%fused_computation.4 | loop fusion | flops 21232512 | bytes 22569984 | tf_op jit(solution)/shard_map/cond/branch_1_fun/reduce_sum | solution.py:94
  237.0 59.2 %all-gather.13.cloned.1.call-done = bf16[512,8192]{1,0:T(8,128)(2,1)} async-done(((bf16[512,512]{1,0:T(8,128)(2,1)}), bf16[512,8192]{1,0:T(8,128)(2,1)}) %all-gather.13.cloned.1.call-update) | async-done | bytes 8388624 | tf_op jit(solution)/shard_map/all_gather | solution.py:111
  296.2 7.8 %convolution_convert_fusion = bf16[288,8192]{1,0:T(8,128)(2,1)} fusion(bf16[512,8192]{1,0:T(8,128)(2,1)} %all-gather.13.cloned.1.call-done, f32[4,288,128]{2,1,0:T(8,128)S(1)} %get-tuple-element.24, f32[4,288]{1,0:T(4,128)S(1)} %get-tuple-element.25), kind=kOutput, calls=%fused_computation.17 | convolution fusion | flops 2418573312 | bytes 13701632 | tf_op jit(solution)/shard_map/dot_general | solution.py:109
  304.1 58.4 %reduce-scatter.2.cloned.1.call-done = bf16[144,8192]{1,0:T(8,128)(2,1)} async-done(((bf16[288,8192]{1,0:T(8,128)(2,1)}), bf16[144,8192]{1,0:T(8,128)(2,1)}) %reduce-scatter.2.cloned.1.call-update) | async-done | bytes 2359312 | tf_op jit(solution)/shard_map/reduce_scatter | solution.py:114
  (80 shorter events, 21.3 us)
Async XLA Ops:
  6.5 56.6 %copy-start.1 = (bf16[512,128]{1,0:T(8,128)(2,1)S(1)}, bf16[512,128]{1,0:T(8,128)(2,1)}, u32[]{:S(2)}) copy-start(bf16[512,128]{1,0:T(8,128)(2,1)} %param.14) | copy-start | bytes 393220
  6.5 56.2 %copy-start.4 = (bf16[128]{0:T(256)(128)(2,1)S(1)}, bf16[128]{0:T(256)(128)(2,1)}, u32[]{:S(2)}) copy-start(bf16[128]{0:T(256)(128)(2,1)} %param.17) | copy-start | bytes 772
  6.5 131.3 %all-gather.9.cloned.1.call-start = ((), (), s32[]{:S(2)}) async-start(), calls=%async_computation.2 | async-start | bytes 2228224 | tf_op jit(solution)/shard_map/all_gather | solution.py:60
  7.3 137.2 %all-gather.7.cloned.1.call-start = ((), (), s32[]{:S(2)}) async-start(), calls=%async_computation.1 | async-start | bytes 8912896 | tf_op jit(solution)/shard_map/all_gather | solution.py:54
  8.0 170.2 %all-gather.15.cloned.1.call-start = ((), (), s32[]{:S(2)}) async-start(), calls=%async_computation.6 | async-start | bytes 1253376 | tf_op jit(solution)/shard_map/all_gather | solution.py:80
  8.1 8.4 %collective-permute-start = (bf16[512,128]{1,0:T(8,128)(2,1)}, bf16[512,128]{1,0:T(8,128)(2,1)S(1)}, u32[]{:S(2)}, u32[]{:S(2)}) collective-permute-start(bf16[512,128]{1,0:T(8,128)(2,1)} %param.14), channel_id=1, source_target_pairs={{0,2},{2,4},{4,6},{6,8},{8,10},{10,12},{12,14},{14,16},{16,18},{18... | collective-permute-start | bytes 393224 | tf_op jit(solution)/shard_map/ppermute | solution.py:20
  16.4 7.2 %collective-permute-start.1 = (bf16[512,128]{1,0:T(8,128)(2,1)S(1)}, bf16[512,128]{1,0:T(8,128)(2,1)S(1)}, u32[]{:S(2)}, u32[]{:S(2)}) collective-permute-start(bf16[512,128]{1,0:T(8,128)(2,1)S(1)} %collective-permute-done), channel_id=1, source_target_pairs={{0,2},{2,4},{4,6},{6,8},{8,10},{10,12},{12,14},{14,16},{16,18},{18... | collective-permute-start | bytes 393224 | tf_op jit(solution)/shard_map/ppermute | solution.py:20
  23.6 8.6 %collective-permute-start.2 = (bf16[512,128]{1,0:T(8,128)(2,1)S(1)}, bf16[512,128]{1,0:T(8,128)(2,1)S(1)}, u32[]{:S(2)}, u32[]{:S(2)}) collective-permute-start(bf16[512,128]{1,0:T(8,128)(2,1)S(1)} %collective-permute-done.1), channel_id=1, source_target_pairs={{0,2},{2,4},{4,6},{6,8},{8,10},{10,12},{12,14},{14,16},{16,18},{18... | collective-permute-start | bytes 393224 | tf_op jit(solution)/shard_map/ppermute | solution.py:20
  32.2 7.1 %collective-permute-start.3 = (bf16[512,128]{1,0:T(8,128)(2,1)S(1)}, bf16[512,128]{1,0:T(8,128)(2,1)S(1)}, u32[]{:S(2)}, u32[]{:S(2)}) collective-permute-start(bf16[512,128]{1,0:T(8,128)(2,1)S(1)} %collective-permute-done.2), channel_id=1, source_target_pairs={{0,2},{2,4},{4,6},{6,8},{8,10},{10,12},{12,14},{14,16},{16,18},{18... | collective-permute-start | bytes 393224 | tf_op jit(solution)/shard_map/ppermute | solution.py:20
  39.3 8.9 %collective-permute-start.4 = (bf16[512,128]{1,0:T(8,128)(2,1)S(1)}, bf16[512,128]{1,0:T(8,128)(2,1)S(1)}, u32[]{:S(2)}, u32[]{:S(2)}) collective-permute-start(bf16[512,128]{1,0:T(8,128)(2,1)S(1)} %collective-permute-done.3), channel_id=1, source_target_pairs={{0,2},{2,4},{4,6},{6,8},{8,10},{10,12},{12,14},{14,16},{16,18},{18... | collective-permute-start | bytes 393224 | tf_op jit(solution)/shard_map/ppermute | solution.py:20
  48.2 7.2 %collective-permute-start.5 = (bf16[512,128]{1,0:T(8,128)(2,1)S(1)}, bf16[512,128]{1,0:T(8,128)(2,1)S(1)}, u32[]{:S(2)}, u32[]{:S(2)}) collective-permute-start(bf16[512,128]{1,0:T(8,128)(2,1)S(1)} %collective-permute-done.4), channel_id=1, source_target_pairs={{0,2},{2,4},{4,6},{6,8},{8,10},{10,12},{12,14},{14,16},{16,18},{18... | collective-permute-start | bytes 393224 | tf_op jit(solution)/shard_map/ppermute | solution.py:20
  55.3 7.1 %collective-permute-start.6 = (bf16[512,128]{1,0:T(8,128)(2,1)S(1)}, bf16[512,128]{1,0:T(8,128)(2,1)S(1)}, u32[]{:S(2)}, u32[]{:S(2)}) collective-permute-start(bf16[512,128]{1,0:T(8,128)(2,1)S(1)} %collective-permute-done.5), channel_id=1, source_target_pairs={{0,2},{2,4},{4,6},{6,8},{8,10},{10,12},{12,14},{14,16},{16,18},{18... | collective-permute-start | bytes 393224 | tf_op jit(solution)/shard_map/ppermute | solution.py:20
  62.4 7.2 %collective-permute-start.7 = (bf16[512,128]{1,0:T(8,128)(2,1)S(1)}, bf16[512,128]{1,0:T(8,128)(2,1)S(1)}, u32[]{:S(2)}, u32[]{:S(2)}) collective-permute-start(bf16[512,128]{1,0:T(8,128)(2,1)S(1)} %collective-permute-done.6), channel_id=1, source_target_pairs={{0,2},{2,4},{4,6},{6,8},{8,10},{10,12},{12,14},{14,16},{16,18},{18... | collective-permute-start | bytes 393224 | tf_op jit(solution)/shard_map/ppermute | solution.py:20
  62.9 71.7 %copy-start = (bf16[288,8192]{1,0:T(8,128)(2,1)S(1)}, bf16[288,8192]{1,0:T(8,128)(2,1)}, u32[]{:S(2)}) copy-start(bf16[288,8192]{1,0:T(8,128)(2,1)} %param.11) | copy-start | bytes 14155780
  69.6 10.0 %collective-permute-start.8 = (bf16[512,128]{1,0:T(8,128)(2,1)S(1)}, bf16[512,128]{1,0:T(8,128)(2,1)S(1)}, u32[]{:S(2)}, u32[]{:S(2)}) collective-permute-start(bf16[512,128]{1,0:T(8,128)(2,1)S(1)} %collective-permute-done.7), channel_id=1, source_target_pairs={{0,2},{2,4},{4,6},{6,8},{8,10},{10,12},{12,14},{14,16},{16,18},{18... | collective-permute-start | bytes 393224 | tf_op jit(solution)/shard_map/ppermute | solution.py:20
  79.6 10.0 %collective-permute-start.9 = (bf16[512,128]{1,0:T(8,128)(2,1)S(1)}, bf16[512,128]{1,0:T(8,128)(2,1)S(1)}, u32[]{:S(2)}, u32[]{:S(2)}) collective-permute-start(bf16[512,128]{1,0:T(8,128)(2,1)S(1)} %collective-permute-done.8), channel_id=1, source_target_pairs={{0,2},{2,4},{4,6},{6,8},{8,10},{10,12},{12,14},{14,16},{16,18},{18... | collective-permute-start | bytes 393224 | tf_op jit(solution)/shard_map/ppermute | solution.py:20
  89.6 7.2 %collective-permute-start.10 = (bf16[512,128]{1,0:T(8,128)(2,1)S(1)}, bf16[512,128]{1,0:T(8,128)(2,1)S(1)}, u32[]{:S(2)}, u32[]{:S(2)}) collective-permute-start(bf16[512,128]{1,0:T(8,128)(2,1)S(1)} %collective-permute-done.9), channel_id=1, source_target_pairs={{0,2},{2,4},{4,6},{6,8},{8,10},{10,12},{12,14},{14,16},{16,18},{18... | collective-permute-start | bytes 393224 | tf_op jit(solution)/shard_map/ppermute | solution.py:20
  96.8 10.0 %collective-permute-start.11 = (bf16[512,128]{1,0:T(8,128)(2,1)S(1)}, bf16[512,128]{1,0:T(8,128)(2,1)S(1)}, u32[]{:S(2)}, u32[]{:S(2)}) collective-permute-start(bf16[512,128]{1,0:T(8,128)(2,1)S(1)} %collective-permute-done.10), channel_id=1, source_target_pairs={{0,2},{2,4},{4,6},{6,8},{8,10},{10,12},{12,14},{14,16},{16,18},{18... | collective-permute-start | bytes 393224 | tf_op jit(solution)/shard_map/ppermute | solution.py:20
  106.9 10.0 %collective-permute-start.12 = (bf16[512,128]{1,0:T(8,128)(2,1)S(1)}, bf16[512,128]{1,0:T(8,128)(2,1)S(1)}, u32[]{:S(2)}, u32[]{:S(2)}) collective-permute-start(bf16[512,128]{1,0:T(8,128)(2,1)S(1)} %collective-permute-done.11), channel_id=1, source_target_pairs={{0,2},{2,4},{4,6},{6,8},{8,10},{10,12},{12,14},{14,16},{16,18},{18... | collective-permute-start | bytes 393224 | tf_op jit(solution)/shard_map/ppermute | solution.py:20
  116.9 7.6 %collective-permute-start.13 = (bf16[512,128]{1,0:T(8,128)(2,1)S(1)}, bf16[512,128]{1,0:T(8,128)(2,1)S(1)}, u32[]{:S(2)}, u32[]{:S(2)}) collective-permute-start(bf16[512,128]{1,0:T(8,128)(2,1)S(1)} %collective-permute-done.12), channel_id=1, source_target_pairs={{0,2},{2,4},{4,6},{6,8},{8,10},{10,12},{12,14},{14,16},{16,18},{18... | collective-permute-start | bytes 393224 | tf_op jit(solution)/shard_map/ppermute | solution.py:20
  124.5 10.1 %collective-permute-start.14 = (bf16[512,128]{1,0:T(8,128)(2,1)S(1)}, bf16[512,128]{1,0:T(8,128)(2,1)S(1)}, u32[]{:S(2)}, u32[]{:S(2)}) collective-permute-start(bf16[512,128]{1,0:T(8,128)(2,1)S(1)} %collective-permute-done.13), channel_id=1, source_target_pairs={{0,2},{2,4},{4,6},{6,8},{8,10},{10,12},{12,14},{14,16},{16,18},{18... | collective-permute-start | bytes 393224 | tf_op jit(solution)/shard_map/ppermute | solution.py:20
  137.7 79.9 %all-gather.11.cloned.1.call-start = ((), (), s32[]{:S(2)}) async-start(), calls=%async_computation.3 | async-start | bytes 1253376 | tf_op jit(solution)/shard_map/all_gather | solution.py:81
  143.0 153.2 %all-gather.13.cloned.1.call-start = ((), (), s32[]{:S(2)}) async-start(), calls=%async_computation.4 | async-start | bytes 8912896 | tf_op jit(solution)/shard_map/all_gather | solution.py:111
  143.6 218.9 %reduce-scatter.2.cloned.1.call-start = ((), (), s32[]{:S(2)}) async-start(), calls=%async_computation.5 | async-start | bytes 7077888 | tf_op jit(solution)/shard_map/reduce_scatter | solution.py:114
  (3 other events, 65.4 us)
Sparse Core Ops, SparseCore 0:
  9.5 46.1 all-gather.8
  57.8 78.5 all-gather.6
  138.7 39.5 all-gather.14
  180.4 37.1 all-gather.10
  219.6 76.5 all-gather.12
  304.2 58.2 reduce-scatter.1
